TPU v7x, 256 devices: a whole 4x4x8 slice. The times are simulated.
256 devices in a mesh: row: 16 (over x, y), col: 16 (over z, core).
Axes of the slice: x: 4, y: 4, z: 8, core: 2. Of those that a mesh axis runs over, the one named last changes fastest.
Arguments:
- panel: float32 [49152, 512], P(('row', 'col')), may hold values from -0.027063294 to 0.027063294
- trailing: float32 [49152, 8192], P('row', 'col'), may hold values from -6 to 6
- counts: int32 [16], P('row'), may hold values from 1 to 6, 56 in all
Outputs:
- upper: float32 [512, 512], replicated
- projected: float32 [512, 8192], P(None, 'col')
Inputs may be any that keep to these rules, and one draw needn't show every extreme that they name: `counts`: the valid tiles of a block are its first ones; some grid row has all 6 valid.
All inputs are finite; a program needn't handle non-finite values.
Results may differ from a plain program's by a relative error of at most 0.0003.
Values sent between devices are 32-bit elements; how exact they have to be, the bound alone decides.
No kernel may reach another device: no remote copies, remote signals or barrier semaphores. Data moves between devices by JAX's collectives and lax.ppermute only.
A program may use at most 64 MiB of HBM per device.

v0:
```python
import jax
import jax.numpy as jnp
from jax import lax
from jax.sharding import PartitionSpec as P


def in_one(arrays, axis):
    ends = [0]
    for a in arrays:
        ends.append(ends[-1] + a.size)
    total = lax.psum(jnp.concatenate([a.ravel() for a in arrays]), axis)
    return tuple((total[b:e].reshape(a.shape) for a, b, e in zip(arrays, ends, ends[1:])))


def inner(left, right):
    return lax.dot_general(
        left,
        right,
        (((0,), (0,)), ((), ())),
        precision=lax.Precision.HIGHEST,
        preferred_element_type=jnp.float32,
    )


def finish(gram, cross):
    lower = jnp.linalg.cholesky(gram)
    solved = lax.linalg.triangular_solve(lower, cross, left_side=True, lower=True)
    return (lower, solved)


def body(panel, trailing, counts):
    width = panel.shape[1]
    valid = counts[0]
    piece = lax.all_gather(panel, "col", axis=0, tiled=True)
    indices = lax.iota(jnp.int32, piece.shape[0])
    keep = (indices // width < valid).astype(jnp.float32)
    piece = piece * keep[:, None]
    gram = inner(piece, piece)
    cross = inner(piece, trailing)
    gram, cross = in_one((gram, cross), "row")
    lower, solved = finish(gram, cross)
    return (lower.T, solved)


def solution(mesh):
    return jax.shard_map(
        body,
        mesh=mesh,
        in_specs=(P(("row", "col"), None), P("row", "col"), P("row")),
        out_specs=(P(), P(None, "col")),
        check_vma=False,
    )
```

profile of v0, /device:TPU:2, one launch (start us, length us, event | category | flops | bytes accessed | tf_op | source)
XLA Modules:
  0.0 350.8 jit_solution(1211601572452920145)
XLA Ops:
  8.6 50.2 %all-gather.2.cloned.1.call-done = f32[3072,512]{1,0:T(8,128)} async-done(((f32[192,512]{1,0:T(8,128)}), f32[3072,512]{1,0:T(8,128)}) %all-gather.2.cloned.1.call-update) | async-done | bytes 6291472 | tf_op jit(solution)/shard_map/all_gather | solution.py:34
  58.8 15.7 %fusion.6 = f32[64,4,8,128]{3,2,1,0:T(8,128)S(1)} fusion(f32[3072,512]{1,0:T(8,128)} %all-gather.2.cloned.1.call-done, f32[3072]{0:T(1024)S(1)} %fusion.45), kind=kOutput, calls=%fused_computation.9 | convolution fusion | flops 9665249280 | bytes 7352320 | tf_op jit(solution)/shard_map/dot_general | solution.py:16
  74.8 23.5 %fusion.9 = f32[64,4,8,128]{3,2,1,0:T(8,128)S(1)} fusion(f32[3072,512]{1,0:T(8,128)} %param.4, f32[3072,512]{1,0:T(8,128)S(1)} %copy-done, f32[3072]{0:T(1024)S(1)} %fusion.45), kind=kOutput, calls=%fused_computation.10 | convolution fusion | flops 9665249280 | bytes 13643776 | tf_op jit(solution)/shard_map/dot_general | solution.py:16
  98.5 1.4 pad_maximum_fusion
  100.0 99.7 %all-reduce.3.cloned.1.call-done = f32[524288]{0:T(1024)} async-done(((f32[524288]{0:T(1024)}), f32[524288]{0:T(1024)}) %all-reduce.3.cloned.1.call-update) | async-done | bytes 2097168 | tf_op jit(solution)/shard_map/psum | solution.py:11
  199.7 1.3 slice.178
  201.7 11.7 %cholesky.104 = f32[128,128]{1,0:T(8,128)S(1)} custom-call(f32[128,128]{1,0:T(8,128)S(1)} %cholesky.266), custom_call_target="Cholesky" | custom-call | tf_op jit(solution)/shard_map/jit(cholesky)/cholesky | solution.py:26
  213.5 9.8 %custom-call.30 = f32[1,128,128]{1,2,0:T(8,128)S(1)} custom-call(f32[1,128,128]{2,1,0:T(8,128)S(1)} %get-tuple-element.39), custom_call_target="InvertDiagBlocksLowerTriangular" | custom-call | tf_op jit(solution)/shard_map/jit(cholesky)/cholesky | solution.py:26
  224.1 11.7 %cholesky.217 = f32[128,128]{1,0:T(8,128)S(1)} custom-call(f32[128,128]{1,0:T(8,128)S(1)} %cholesky.270), custom_call_target="Cholesky" | custom-call | tf_op jit(solution)/shard_map/jit(cholesky)/cholesky | solution.py:26
  235.9 10.2 %custom-call.31 = f32[1,128,128]{1,2,0:T(8,128)S(1)} custom-call(f32[1,128,128]{2,1,0:T(8,128)S(1)} %get-tuple-element.36), custom_call_target="InvertDiagBlocksLowerTriangular" | custom-call | tf_op jit(solution)/shard_map/jit(cholesky)/cholesky | solution.py:26
  246.7 11.7 %cholesky.238 = f32[128,128]{1,0:T(8,128)S(1)} custom-call(f32[128,128]{1,0:T(8,128)S(1)} %cholesky.275), custom_call_target="Cholesky" | custom-call | tf_op jit(solution)/shard_map/jit(cholesky)/cholesky | solution.py:26
  259.1 9.8 %custom-call.32 = f32[1,128,128]{1,2,0:T(8,128)S(1)} custom-call(f32[1,128,128]{2,1,0:T(8,128)S(1)} %get-tuple-element.33), custom_call_target="InvertDiagBlocksLowerTriangular" | custom-call | tf_op jit(solution)/shard_map/jit(cholesky)/cholesky | solution.py:26
  269.5 11.9 %cholesky.255 = f32[128,128]{1,0:T(8,128)S(1)} custom-call(f32[128,128]{1,0:T(8,128)S(1)} %convolution_subtract_fusion.5), custom_call_target="Cholesky" | custom-call | tf_op jit(solution)/shard_map/jit(cholesky)/cholesky | solution.py:26
  285.5 8.0 %while.1 = (s32[]{:T(128)}, f32[512,512]{1,0:T(8,128)S(1)}, s32[4,2]{0,1:T(2,128)S(1)}, f32[4,128,128]{2,1,0:T(8,128)S(1)}, s32[]{:T(128)}) while((s32[]{:T(128)}, f32[512,512]{1,0:T(8,128)S(1)}, s32[4,2]{0,1:T(2,128)S(1)}, f32[4,128,128]{2,1,0:T(8,128)S(1)}, s32[]{:T(128)}) %tuple.37), condition=%wide.while_cond, body=%wide.while_body.sunk | while | flops 2 | bytes 131181 | solution.py:27
  286.1 1.4 bitcast_dynamic-update-slice_fusion.2
  288.1 1.4 bitcast_dynamic-update-slice_fusion.2
  290.2 1.4 bitcast_dynamic-update-slice_fusion.2
  292.2 1.4 bitcast_dynamic-update-slice_fusion.2
  293.6 39.9 %custom-call.33 = f32[4,128,128]{1,2,0:T(8,128)} custom-call(f32[4,128,128]{2,1,0:T(8,128)S(1)} %get-tuple-element.9), custom_call_target="InvertDiagBlocksLowerTriangular" | custom-call | tf_op jit(solution)/shard_map/triangular_solve | solution.py:27
  333.5 1.3 fusion.49
  336.5 1.3 fusion.34
  338.3 1.3 fusion.32
  340.2 1.3 fusion.31
  342.5 1.3 copy.8
  (50 shorter events, 12.7 us)
Async XLA Ops:
  7.2 51.7 %all-gather.2.cloned.1.call-start = ((), (), s32[]{:S(2)}) async-start(), calls=%async_computation | async-start | bytes 6684672 | tf_op jit(solution)/shard_map/all_gather | solution.py:34
  7.9 191.8 %all-reduce.3.cloned.1.call-start = ((), (), s32[]{:S(2)}) async-start(), calls=%async_computation.1 | async-start | bytes 4194304 | tf_op jit(solution)/shard_map/psum | solution.py:11
  58.8 16.0 %copy-start = (f32[3072,512]{1,0:T(8,128)S(1)}, f32[3072,512]{1,0:T(8,128)}, u32[]{:S(2)}) copy-start(f32[3072,512]{1,0:T(8,128)} %all-gather.2.cloned.1.call-done) | copy-start | bytes 18874372
Sparse Core Ops, SparseCore 0:
  9.8 48.9 all-gather.1
  100.1 99.5 all-reduce.2
where the time goes:
time: 355 us; the launch traced here: 351 us
  waiting for transfers between devices  151 us (43%)
  other arithmetic  122 us (34%)
  matrix products  47.5 us (13%)
  between operations  17.7 us (5%)
  local copies, waits for them, and re-layouts  13.1 us (4%)
    psum x1, waiting for transfers between devices, in_one(): total = lax.psum(jnp.concatenate([a.ravel() for a in arrays]), axis)  99.7 us
    another operation x14, other arithmetic, finish(): lower = jnp.linalg.cholesky(gram)  78.9 us
    all_gather x1, waiting for transfers between devices, body(): piece = lax.all_gather(panel, 'col', axis=0, tiled=True)  50.2 us
    another operation x4, other arithmetic, finish(): lax.linalg.triangular_solve(lower, cross, left_side=True, lower=True)  41.2 us
    dot_general x2, matrix products, inner(): lax.dot_general(left, right, (((0,), (0,)), ((), ())), precision=lax.Prec...  39.1 us
    another operation x12, local copies, waits for them, and re-layouts  7.92 us
  transfers between devices with their start and end apart: 2, of which 2 were waited for; matrix products, arithmetic and copies ran while one was open for 0% of the time, Pallas kernels for 0%

commit v1 on v0

v1 whole, which is shorter than its diff:
```python
import functools

import jax
import jax.numpy as jnp
from jax import lax
from jax.experimental import pallas as pl
from jax.experimental.pallas import tpu as pltpu
from jax.sharding import PartitionSpec as P

HIGHEST = lax.Precision.HIGHEST
VMEM = pl.BlockSpec(memory_space=pltpu.VMEM)
SMEM = pl.BlockSpec(memory_space=pltpu.SMEM)
BLOCK = 128


def exact_dot(left, right):
    return lax.dot_general(
        left, right, (((1,), (0,)), ((), ())), precision=HIGHEST, preferred_element_type=jnp.float32
    )


def split(value):
    high = value.astype(jnp.bfloat16)
    return high, (value - high.astype(jnp.float32)).astype(jnp.bfloat16)


def upper_blocks(width):
    count = width // BLOCK
    return [(i, j) for i in range(count) for j in range(i, count)]


def gram_kernel(place_ref, panel_ref, out_ref):
    rows, width = panel_ref.shape
    index = place_ref[0] * rows + lax.broadcasted_iota(jnp.int32, (rows, 1), 0)
    masked = jnp.where(index < place_ref[1] * width, panel_ref[...], 0.0)
    flipped = masked.T
    at = 0
    for i in range(width // BLOCK):
        start = i * BLOCK
        strip = exact_dot(flipped[start : start + BLOCK, :], masked[:, start:])
        for j in range((width - start) // BLOCK):
            out_ref[at : at + BLOCK, :] = strip[:, j * BLOCK : (j + 1) * BLOCK]
            at += BLOCK


def gram(place, panel):
    blocks = len(upper_blocks(panel.shape[1]))
    return pl.pallas_call(
        gram_kernel,
        out_shape=jax.ShapeDtypeStruct((blocks * BLOCK, BLOCK), jnp.float32),
        in_specs=[SMEM, VMEM],
        out_specs=VMEM,
        name="gram",
    )(place, panel)


def eliminate(e):
    rows = len(e)
    sub = lax.broadcasted_iota(jnp.int32, e[0].shape, 0)
    for g in range(rows):
        cols = [[None] * rows for _ in range(8)]
        for j in range(8):
            for v in range(g, rows):
                at = 8 * g + j
                cols[j][v] = jnp.broadcast_to(e[v][:, at : at + 1], (8, 128))
        for k in range(8):
            scale = lax.rsqrt(cols[k][g][k : k + 1, :])
            wide = jnp.concatenate([scale] * (e[0].shape[1] // 128), axis=1)
            pivot = e[g][k : k + 1, :] * wide
            tops = [cols[j][g][k : k + 1, :] * scale for j in range(k + 1, 8)]
            for v in range(g, rows):
                m = cols[k][v] * scale
                if v == g:
                    m = jnp.where(sub[:, :128] > k, m, 0.0)
                    e[v] = jnp.where(sub == k, pivot, e[v])
                many = jnp.concatenate([m] * (e[0].shape[1] // 128), axis=1)
                e[v] = e[v] - many * pivot
                for j in range(k + 1, 8):
                    cols[j][v] = cols[j][v] - m * tops[j - k - 1]
    return e


def factor_kernel(packed_ref, upper_ref, inverse_ref):
    width = upper_ref.shape[0]
    count = width // BLOCK
    work = {}
    for at, key in enumerate(upper_blocks(width)):
        work[key] = packed_ref[at * BLOCK : (at + 1) * BLOCK, :]
    upper_ref[...] = jnp.zeros_like(upper_ref)
    inverse_ref[...] = jnp.zeros_like(inverse_ref)
    row = lax.broadcasted_iota(jnp.int32, (BLOCK, BLOCK), 0)
    column = lax.broadcasted_iota(jnp.int32, (BLOCK, BLOCK), 1)
    eye = (row == column).astype(jnp.float32)
    for s in range(count):
        here = slice(s * BLOCK, (s + 1) * BLOCK)
        if s == 0:
            diagonal = packed_ref[:BLOCK, :]
        else:
            diagonal = work_diagonal
        both = jnp.concatenate([diagonal, eye], axis=1)
        both = jnp.concatenate(eliminate([both[8 * v : 8 * v + 8, :] for v in range(BLOCK // 8)]), axis=0)
        inverse = both[:, BLOCK:]
        upper_ref[here, here] = jnp.where(row <= column, both[:, :BLOCK], 0.0)
        left = None
        if s:
            left = exact_dot(inverse, inverse_ref[here, : s * BLOCK])
            inverse_ref[here, : s * BLOCK] = left
        inverse_ref[here, here] = inverse
        if s + 1 < count:
            strip = jnp.concatenate([work[s, j] for j in range(s + 1, count)], axis=1)
            strip = exact_dot(inverse, strip)
            upper_ref[here, (s + 1) * BLOCK :] = strip
            flipped = strip.T
            for i in range(s + 1, count):
                part = flipped[(i - s - 1) * BLOCK : (i - s) * BLOCK, :]
                change = exact_dot(part, strip[:, (i - s - 1) * BLOCK :])
                for j in range(i, count):
                    work[i, j] = work[i, j] - change[:, (j - i) * BLOCK : (j - i + 1) * BLOCK]
                there = slice(i * BLOCK, (i + 1) * BLOCK)
                inverse_ref[there, here] = -exact_dot(part, inverse)
                if s:
                    inverse_ref[there, : s * BLOCK] -= exact_dot(part, left)
            work_diagonal = work[s + 1, s + 1]


def factor(packed, width):
    return pl.pallas_call(
        factor_kernel,
        out_shape=[jax.ShapeDtypeStruct((width, width), jnp.float32)] * 2,
        in_specs=[VMEM],
        out_specs=[VMEM, VMEM],
        cost_estimate=pl.CostEstimate(flops=20_000_000_000, bytes_accessed=3 << 20, transcendentals=512),
        name="factor",
    )(packed)


def cross_kernel(valid_ref, piece_ref, trailing_ref, out_ref):
    step = pl.program_id(0)

    @pl.when(step == 0)
    def _():
        out_ref[...] = jnp.zeros_like(out_ref)

    @pl.when(step < valid_ref[0])
    def _():
        left = split(piece_ref[...])
        right = split(trailing_ref[...])

        def product(a, b):
            return lax.dot_general(a, b, (((0,), (0,)), ((), ())), preferred_element_type=jnp.float32)

        out_ref[...] += product(left[0], right[0]) + (product(left[0], right[1]) + product(left[1], right[0]))


def cross(valid, piece, trailing):
    rows, width = piece.shape
    columns = trailing.shape[1]
    return pl.pallas_call(
        cross_kernel,
        grid=(rows // width,),
        out_shape=jax.ShapeDtypeStruct((width, columns), jnp.float32),
        in_specs=[
            SMEM,
            pl.BlockSpec((width, width), lambda i: (i, 0)),
            pl.BlockSpec((width, columns), lambda i: (i, 0)),
        ],
        out_specs=pl.BlockSpec((width, columns), lambda i: (0, 0)),
        name="cross",
    )(valid, piece, trailing)


def apply_kernel(inverse_ref, total_ref, out_ref):
    width = inverse_ref.shape[0]
    right = split(total_ref[...])
    for i in range(width // BLOCK):
        here, known = slice(i * BLOCK, (i + 1) * BLOCK), (i + 1) * BLOCK
        left = split(inverse_ref[here, :known])

        def product(a, b):
            return lax.dot_general(a, b[:known, :], (((1,), (0,)), ((), ())), preferred_element_type=jnp.float32)

        out_ref[here, :] = product(left[0], right[0]) + (product(left[0], right[1]) + product(left[1], right[0]))


def apply(inverse, total):
    return pl.pallas_call(
        apply_kernel,
        out_shape=jax.ShapeDtypeStruct(total.shape, jnp.float32),
        in_specs=[VMEM, VMEM],
        out_specs=VMEM,
        name="apply",
    )(inverse, total)


def exchange(blocks, axis, groups=None):
    return lax.all_to_all(blocks, axis, 0, 0, tiled=True, axis_index_groups=groups)


def spread(block, count):
    return jnp.broadcast_to(block[None], (count, *block.shape))


def body(rows, cols, panel, trailing, counts):
    width = panel.shape[1]
    place = jnp.stack([lax.axis_index("col"), counts[0]])
    piece = lax.all_gather(panel, "col", axis=0, tiled=True)

    lines = cols // 2
    planes = [[r * cols + 2 * z + k for r in range(rows) for k in range(2)] for z in range(lines)]
    uprights = [[2 * z + k for z in range(lines)] for k in range(2)]
    both = ("row", "col")
    packed = gram(place, panel)
    shares = exchange(packed.reshape(2 * rows, -1, BLOCK), both, planes)
    shares = jnp.sum(shares, axis=0)
    shares = jnp.sum(exchange(spread(shares, lines), "col", uprights), axis=0)
    packed = exchange(spread(shares, 2 * rows), both, planes).reshape(packed.shape)
    upper, inverse = factor(packed, width)

    total = cross(counts, piece, trailing)
    total = jnp.sum(exchange(total.reshape(rows, -1, total.shape[1]), "row"), axis=0)
    total = exchange(spread(total, rows), "row").reshape(width, -1)
    return upper, apply(inverse, total)


def solution(mesh):
    return jax.shard_map(
        functools.partial(body, mesh.shape["row"], mesh.shape["col"]),
        mesh=mesh,
        in_specs=(P(("row", "col"), None), P("row", "col"), P("row")),
        out_specs=(P(), P(None, "col")),
        check_vma=False,
    )
```

time: 355 us -> 153 us (0.43)
  other arithmetic: 122 us -> 0.72 us
  waiting for transfers between devices: 151 us -> 49.8 us
  matrix products: 47.5 us -> 0 us
  Pallas kernels: 0 us -> 36.4 us
  starting transfers between devices: 0.08 us -> 26.8 us
  blocking collectives: 0 us -> 18.4 us
  local copies, waits for them, and re-layouts: 13.1 us -> 3.77 us
    another operation x18 -> x1, other arithmetic: 120 us -> 0.59 us  [body(): place = jnp.stack([lax.axis_index('col'), counts[0]])]
    psum x1 -> x0, waiting for transfers between devices: 99.7 us -> none  [in_one(): total = lax.psum(jnp.concatenate([a.ravel() for a in arrays]), axis)]
    dot_general x2 -> x0, matrix products: 39.1 us -> none  [inner(): lax.dot_general(left, right, (((0,), (0,)), ((), ())), precision=lax.Prec...]
    pallas_call x0 -> x4, Pallas kernels: none -> 36.4 us  [the longest x1 20.4 us: factor(): pl.pallas_call(factor_kernel, out_shape=[jax.ShapeDtypeStruct((width, wid...]
    all_gather x1, waiting for transfers between devices: 50.2 us -> 22.9 us  [body(): piece = lax.all_gather(panel, 'col', axis=0, tiled=True)]
    all_to_all x0 -> x4, starting transfers between devices: none -> 26.8 us  [exchange(): lax.all_to_all(blocks, axis, 0, 0, tiled=True, axis_index_groups=groups)]
    all_to_all x0 -> x4, waiting for transfers between devices: none -> 26.2 us  [exchange(): lax.all_to_all(blocks, axis, 0, 0, tiled=True, axis_index_groups=groups)]
    all_to_all x0 -> x1, blocking collectives: none -> 18.4 us  [exchange(): lax.all_to_all(blocks, axis, 0, 0, tiled=True, axis_index_groups=groups)]
  transfers between devices with their start and end apart: 2 -> 5, of which waited for: 2 -> 3; matrix products, arithmetic and copies ran while one was open for 0% -> 1% of each run, Pallas kernels for 0% -> 22%
where the time goes in v1:
time: 153 us; the launch traced here: 151 us
  waiting for transfers between devices  49.8 us (33%)
  Pallas kernels  36.4 us (24%)
  starting transfers between devices  26.8 us (18%)
  blocking collectives  18.4 us (12%)
  between operations  14.7 us (10%)
  local copies, waits for them, and re-layouts  3.77 us (2%)
    all_to_all x4, starting transfers between devices, exchange(): lax.all_to_all(blocks, axis, 0, 0, tiled=True, axis_index_groups=groups)  26.8 us
    all_to_all x4, waiting for transfers between devices, exchange(): lax.all_to_all(blocks, axis, 0, 0, tiled=True, axis_index_groups=groups)  26.2 us
    all_gather x1, waiting for transfers between devices, body(): piece = lax.all_gather(panel, 'col', axis=0, tiled=True)  22.9 us
    pallas_call x1, Pallas kernels, factor(): pl.pallas_call(factor_kernel, out_shape=[jax.ShapeDtypeStruct((width, wid...  20.4 us
    all_to_all x1, blocking collectives, exchange(): lax.all_to_all(blocks, axis, 0, 0, tiled=True, axis_index_groups=groups)  18.4 us
    pallas_call x1, Pallas kernels, cross(): pl.pallas_call(cross_kernel, grid=(rows // width,), out_shape=jax.ShapeDt...  10 us
    pallas_call x1, Pallas kernels, apply(): pl.pallas_call(apply_kernel, out_shape=jax.ShapeDtypeStruct(total.shape,...  3.28 us
  transfers between devices with their start and end apart: 5, of which 3 were waited for; matrix products, arithmetic and copies ran while one was open for 1% of the time, Pallas kernels for 22%

profile of v1, /device:TPU:2, one launch (start us, length us, event | category | flops | bytes accessed | tf_op | source)
XLA Modules:
  0.0 150.7 jit_solution(12438237826440255959)
XLA Ops:
  7.2 0.0 all-gather.2.cloned.1.call-start
  7.2 0.7 all-gather.2.cloned.1.call-update
  8.5 0.6 pad_add_fusion.place_ref
  9.1 2.7 %gram.1 = f32[1280,128]{1,0:T(8,128)} custom-call(s32[2]{0:T(128)} %pad_add_fusion.place_ref, f32[192,512]{1,0:T(8,128)} %panel_ref.1), custom_call_target="tpu_custom_call" | custom-call | tf_op jit(solution)/shard_map/gram/pallas_call | solution.py:48
  11.8 18.4 %all_to_all.25 = f32[32,40,128]{2,1,0:T(8,128)S(1)} all-to-all(f32[32,40,128]{2,1,0:T(8,128)} %bitcast.7), channel_id=1, replica_groups={{0,1,16,17,32,33,48,49,64,65,80,81,96,97,112,113,128,129,144,145,160,16..., dimensions={0} | all-to-all | bytes 1310720 | tf_op jit(solution)/shard_map/all_to_all | solution.py:196
  30.3 0.1 reduce_sum.27
  30.3 0.7 broadcast_in_dim.6
  31.0 8.5 %all-to-all-start.1 = ((f32[8,40,128]{2,1,0:T(8,128)}), f32[8,40,128]{2,1,0:T(8,128)S(1)}, u32[]{:S(2)}, u32[]{:S(2)}) async-start(f32[8,40,128]{2,1,0:T(8,128)} %broadcast_in_dim.6), calls=%async_computation.1 | async-start | bytes 327680 | tf_op jit(solution)/shard_map/all_to_all | solution.py:196
  39.5 22.9 %all-gather.2.cloned.1.call-done.piece_ref = f32[3072,512]{1,0:T(8,128)} async-done(((f32[192,512]{1,0:T(8,128)}), f32[3072,512]{1,0:T(8,128)}) %all-gather.2.cloned.1.call-update) | async-done | bytes 6291472 | tf_op jit(solution)/shard_map/all_gather | solution.py:206
  62.3 10.0 %cross.1 = f32[512,512]{1,0:T(8,128)} custom-call(s32[1]{0:T(128)S(6)} %copy.5.valid_ref, f32[3072,512]{1,0:T(8,128)} %all-gather.2.cloned.1.call-done.piece_ref, f32[3072,512]{1,0:T(8,128)} %trailing_ref.1), custom_call_target="tpu_custom_call" | custom-call | tf_op jit(solution)/shard_map/cross/pallas_call | solution.py:158
  72.4 0.0 all-to-all-done.1
  72.4 6.3 %all-to-all-start.3 = ((f32[16,32,512]{2,1,0:T(8,128)}), f32[16,32,512]{2,1,0:T(8,128)S(1)}, u32[]{:S(2)}, u32[]{:S(2)}) async-start(f32[16,32,512]{2,1,0:T(8,128)} %bitcast.6), calls=%async_computation.3 | async-start | bytes 2097152 | tf_op jit(solution)/shard_map/all_to_all | solution.py:196
  78.6 15.4 %all-to-all-done.3 = f32[16,32,512]{2,1,0:T(8,128)S(1)} async-done(((f32[16,32,512]{2,1,0:T(8,128)}), f32[16,32,512]{2,1,0:T(8,128)S(1)}, u32[]{:S(2)}, u32[]{:S(2)}) %all-to-all-start.3) | async-done | bytes 1048608 | tf_op jit(solution)/shard_map/all_to_all | solution.py:196
  94.1 0.9 broadcast_in_dim.7
  95.0 6.4 %all-to-all-start.2 = ((f32[32,40,128]{2,1,0:T(8,128)}), f32[32,40,128]{2,1,0:T(8,128)S(1)}, u32[]{:S(2)}, u32[]{:S(2)}) async-start(f32[32,40,128]{2,1,0:T(8,128)} %broadcast_in_dim.7), calls=%async_computation.2 | async-start | bytes 1310720 | tf_op jit(solution)/shard_map/all_to_all | solution.py:196
  101.4 0.1 reduce_sum.29
  101.5 10.8 %all-to-all-done.2 = f32[32,40,128]{2,1,0:T(8,128)S(1)} async-done(((f32[32,40,128]{2,1,0:T(8,128)}), f32[32,40,128]{2,1,0:T(8,128)S(1)}, u32[]{:S(2)}, u32[]{:S(2)}) %all-to-all-start.2) | async-done | bytes 655392 | tf_op jit(solution)/shard_map/all_to_all | solution.py:196
  112.3 1.2 broadcast_in_dim.8
  113.5 5.7 %all-to-all-start.4 = ((f32[16,32,512]{2,1,0:T(8,128)}), f32[16,32,512]{2,1,0:T(8,128)S(1)}, u32[]{:S(2)}, u32[]{:S(2)}) async-start(f32[16,32,512]{2,1,0:T(8,128)} %broadcast_in_dim.8), calls=%async_computation.4 | async-start | bytes 2097152 | tf_op jit(solution)/shard_map/all_to_all | solution.py:196
  119.1 0.0 copy-done.1
  119.1 20.4 %factor.1 = (f32[512,512]{1,0:T(8,128)}, f32[512,512]{1,0:T(8,128)}) custom-call(f32[1280,128]{1,0:T(8,128)} %bitcast.8), custom_call_target="tpu_custom_call" | custom-call | flops 20000000000 | bytes 3145728 | tf_op jit(solution)/shard_map/factor/pallas_call | solution.py:127
  139.5 0.0 all-to-all-done.4
  139.5 1.0 copy-done
  140.6 3.3 %apply.1 = f32[512,512]{1,0:T(8,128)} custom-call(f32[512,512]{1,0:T(8,128)} %get-tuple-element.5.inverse_ref, f32[512,512]{1,0:T(8,128)} %bitcast.5), custom_call_target="tpu_custom_call" | custom-call | tf_op jit(solution)/shard_map/apply/pallas_call | solution.py:186
  (3 shorter events, 0.0 us)
Async XLA Ops:
  7.2 55.2 %all-gather.2.cloned.1.call-start = ((), (), s32[]{:S(2)}) async-start(), calls=%async_computation.5 | async-start | bytes 6684672 | tf_op jit(solution)/shard_map/all_gather | solution.py:206
  31.0 41.4 %all-to-all-start.1 = ((f32[8,40,128]{2,1,0:T(8,128)}), f32[8,40,128]{2,1,0:T(8,128)S(1)}, u32[]{:S(2)}, u32[]{:S(2)}) async-start(f32[8,40,128]{2,1,0:T(8,128)} %broadcast_in_dim.6), calls=%async_computation.1 | async-start | bytes 327680 | tf_op jit(solution)/shard_map/all_to_all | solution.py:196
  72.4 21.7 %all-to-all-start.3 = ((f32[16,32,512]{2,1,0:T(8,128)}), f32[16,32,512]{2,1,0:T(8,128)S(1)}, u32[]{:S(2)}, u32[]{:S(2)}) async-start(f32[16,32,512]{2,1,0:T(8,128)} %bitcast.6), calls=%async_computation.3 | async-start | bytes 2097152 | tf_op jit(solution)/shard_map/all_to_all | solution.py:196
  95.0 17.3 %all-to-all-start.2 = ((f32[32,40,128]{2,1,0:T(8,128)}), f32[32,40,128]{2,1,0:T(8,128)S(1)}, u32[]{:S(2)}, u32[]{:S(2)}) async-start(f32[32,40,128]{2,1,0:T(8,128)} %broadcast_in_dim.7), calls=%async_computation.2 | async-start | bytes 1310720 | tf_op jit(solution)/shard_map/all_to_all | solution.py:196
  112.3 6.8 %copy-start.1 = (f32[32,40,128]{2,1,0:T(8,128)}, f32[32,40,128]{2,1,0:T(8,128)S(1)}, u32[]{:S(2)}) copy-start(f32[32,40,128]{2,1,0:T(8,128)S(1)} %all-to-all-done.2) | copy-start | bytes 1966084
  113.5 26.1 %all-to-all-start.4 = ((f32[16,32,512]{2,1,0:T(8,128)}), f32[16,32,512]{2,1,0:T(8,128)S(1)}, u32[]{:S(2)}, u32[]{:S(2)}) async-start(f32[16,32,512]{2,1,0:T(8,128)} %broadcast_in_dim.8), calls=%async_computation.4 | async-start | bytes 2097152 | tf_op jit(solution)/shard_map/all_to_all | solution.py:196
  139.5 1.0 copy-start
Sparse Core Ops, SparseCore 0:
  9.8 52.4 all-gather.1

commit v2 on v1

--- a/solution.py
+++ b/solution.py
@@ -214,6 +214,7 @@
     shares = jnp.sum(shares, axis=0)
     shares = jnp.sum(exchange(spread(shares, lines), "col", uprights), axis=0)
     packed = exchange(spread(shares, 2 * rows), both, planes).reshape(packed.shape)
+    piece, packed = lax.optimization_barrier((piece, packed))
     upper, inverse = factor(packed, width)
 
     total = cross(counts, piece, trailing)

time: 153 us -> 137 us (0.90); the launches traced: 151 us -> 137 us
  blocking collectives: 18.4 us -> 77.5 us
  waiting for transfers between devices: 49.8 us -> 0.68 us
  starting transfers between devices: 26.8 us -> 5.9 us
  Pallas kernels: 36.4 us -> 34.8 us
  local copies, waits for them, and re-layouts: 3.77 us -> 2.19 us
    all_to_all x1 -> x4, blocking collectives: 18.4 us -> 77.5 us  [exchange(): lax.all_to_all(blocks, axis, 0, 0, tiled=True, axis_index_groups=groups)]
    all_to_all x4 -> x1, waiting for transfers between devices: 26.2 us -> 0.01 us  [exchange(): lax.all_to_all(blocks, axis, 0, 0, tiled=True, axis_index_groups=groups)]
    all_gather x1, waiting for transfers between devices: 22.9 us -> 0.01 us  [body(): piece = lax.all_gather(panel, 'col', axis=0, tiled=True)]
    all_to_all x4 -> x1, starting transfers between devices: 26.8 us -> 5.86 us  [exchange(): lax.all_to_all(blocks, axis, 0, 0, tiled=True, axis_index_groups=groups)]
    pallas_call x1, Pallas kernels: 10 us -> 8.39 us  [cross(): pl.pallas_call(cross_kernel, grid=(rows // width,), out_shape=jax.ShapeDt...]
    broadcast_in_dim x3, local copies, waits for them, and re-layouts: 2.74 us -> 1.16 us  [spread(): return jnp.broadcast_to(block[None], (count, *block.shape))]
  transfers between devices with their start and end apart: 5 -> 2, of which waited for: 3 -> 0; matrix products, arithmetic and copies ran while one was open for 1% -> 1% of each run, Pallas kernels for 22% -> 17%
where the time goes in v2:
time: 137 us
  blocking collectives  77.5 us (57%)
  Pallas kernels  34.8 us (25%)
  between operations  14.7 us (11%)
  starting transfers between devices  5.9 us (4%)
  local copies, waits for them, and re-layouts  2.19 us (2%)
    all_to_all x4, blocking collectives, exchange(): lax.all_to_all(blocks, axis, 0, 0, tiled=True, axis_index_groups=groups)  77.5 us
    pallas_call x1, Pallas kernels, factor(): pl.pallas_call(factor_kernel, out_shape=[jax.ShapeDtypeStruct((width, wid...  20.4 us
    pallas_call x1, Pallas kernels, cross(): pl.pallas_call(cross_kernel, grid=(rows // width,), out_shape=jax.ShapeDt...  8.39 us
    all_to_all x1, starting transfers between devices, exchange(): lax.all_to_all(blocks, axis, 0, 0, tiled=True, axis_index_groups=groups)  5.86 us
    pallas_call x1, Pallas kernels, apply(): pl.pallas_call(apply_kernel, out_shape=jax.ShapeDtypeStruct(total.shape,...  3.28 us
  transfers between devices with their start and end apart: 2, of which 0 were waited for; matrix products, arithmetic and copies ran while one was open for 1% of the time, Pallas kernels for 17%

profile of v2, /device:TPU:2, one launch (start us, length us, event | category | flops | bytes accessed | tf_op | source)
XLA Modules:
  0.0 136.5 jit_solution(5258550271555809111)
XLA Ops:
  7.2 0.0 all-gather.2.cloned.1.call-start
  7.2 0.7 all-gather.2.cloned.1.call-update
  8.5 0.6 pad_add_fusion.place_ref
  9.1 2.7 %gram.1 = f32[1280,128]{1,0:T(8,128)} custom-call(s32[2]{0:T(128)} %pad_add_fusion.place_ref, f32[192,512]{1,0:T(8,128)} %panel_ref.1), custom_call_target="tpu_custom_call" | custom-call | tf_op jit(solution)/shard_map/gram/pallas_call | solution.py:48
  11.8 18.4 %all_to_all.25 = f32[32,40,128]{2,1,0:T(8,128)S(1)} all-to-all(f32[32,40,128]{2,1,0:T(8,128)} %bitcast.7), channel_id=1, replica_groups={{0,1,16,17,32,33,48,49,64,65,80,81,96,97,112,113,128,129,144,145,160,16..., dimensions={0} | all-to-all | bytes 1310720 | tf_op jit(solution)/shard_map/all_to_all | solution.py:196
  30.3 0.1 reduce_sum.27
  30.3 21.0 %all_to_all.26 = f32[8,40,128]{2,1,0:T(8,128)S(1)} all-to-all(f32[8,40,128]{2,1,0:T(8,128)S(1)} %broadcast_in_dim.6), channel_id=1, replica_groups={{0,2,4,6,8,10,12,14},{1,3,5,7,9,11,13,15},{16,18,20,22,24,26,28,30},{17..., dimensions={0} | all-to-all | bytes 327680 | tf_op jit(solution)/shard_map/all_to_all | solution.py:196
  51.4 16.1 %all_to_all.27 = f32[32,40,128]{2,1,0:T(8,128)} all-to-all(f32[32,40,128]{2,1,0:T(8,128)S(1)} %broadcast_in_dim.7), channel_id=1, replica_groups={{0,1,16,17,32,33,48,49,64,65,80,81,96,97,112,113,128,129,144,145,160,16..., dimensions={0} | all-to-all | bytes 1310720 | tf_op jit(solution)/shard_map/all_to_all | solution.py:196
  67.5 0.0 all-gather.2.cloned.1.call-done.piece_ref
  67.5 8.4 %cross.1 = f32[512,512]{1,0:T(8,128)} custom-call(s32[1]{0:T(128)S(6)} %copy.5.valid_ref, f32[3072,512]{1,0:T(8,128)} %all-gather.2.cloned.1.call-done.piece_ref, f32[3072,512]{1,0:T(8,128)} %trailing_ref.1), custom_call_target="tpu_custom_call" | custom-call | tf_op jit(solution)/shard_map/cross/pallas_call | solution.py:158
  75.9 22.0 %all_to_all.28 = f32[16,32,512]{2,1,0:T(8,128)S(1)} all-to-all(f32[16,32,512]{2,1,0:T(8,128)} %bitcast.6), channel_id=1, replica_groups=mesh['row'=16,'col'=16] {'row'}, dimensions={0} | all-to-all | bytes 2097152 | tf_op jit(solution)/shard_map/all_to_all | solution.py:196
  97.9 0.1 reduce_sum.29
  97.9 1.1 broadcast_in_dim.8
  99.0 5.9 %all-to-all-start.4 = ((f32[16,32,512]{2,1,0:T(8,128)}), f32[16,32,512]{2,1,0:T(8,128)S(1)}, u32[]{:S(2)}, u32[]{:S(2)}) async-start(f32[16,32,512]{2,1,0:T(8,128)} %broadcast_in_dim.8), calls=%async_computation.4 | async-start | bytes 2097152 | tf_op jit(solution)/shard_map/all_to_all | solution.py:196
  104.9 20.4 %factor.1 = (f32[512,512]{1,0:T(8,128)}, f32[512,512]{1,0:T(8,128)}) custom-call(f32[1280,128]{1,0:T(8,128)} %bitcast.8), custom_call_target="tpu_custom_call" | custom-call | flops 20000000000 | bytes 3145728 | tf_op jit(solution)/shard_map/factor/pallas_call | solution.py:127
  125.3 0.0 all-to-all-done.4
  125.3 0.0 copy-start
  125.4 1.0 copy-done
  126.4 3.3 %apply.1 = f32[512,512]{1,0:T(8,128)} custom-call(f32[512,512]{1,0:T(8,128)} %get-tuple-element.8.inverse_ref, f32[512,512]{1,0:T(8,128)} %bitcast.5), custom_call_target="tpu_custom_call" | custom-call | tf_op jit(solution)/shard_map/apply/pallas_call | solution.py:186
  (3 shorter events, 0.1 us)
Async XLA Ops:
  7.2 60.3 %all-gather.2.cloned.1.call-start = ((), (), s32[]{:S(2)}) async-start(), calls=%async_computation.5 | async-start | bytes 6684672 | tf_op jit(solution)/shard_map/all_gather | solution.py:206
  99.0 26.3 %all-to-all-start.4 = ((f32[16,32,512]{2,1,0:T(8,128)}), f32[16,32,512]{2,1,0:T(8,128)S(1)}, u32[]{:S(2)}, u32[]{:S(2)}) async-start(f32[16,32,512]{2,1,0:T(8,128)} %broadcast_in_dim.8), calls=%async_computation.4 | async-start | bytes 2097152 | tf_op jit(solution)/shard_map/all_to_all | solution.py:196
  125.3 1.0 copy-start
Sparse Core Ops, SparseCore 0:
  9.8 52.4 all-gather.1
